TPU v7x, 32 devices: a whole 2x2x4 slice. The times are simulated.
32 devices in a mesh: pole: 4 (over x, core), row: 4 (over z), col: 2 (over y).
Axes of the slice: x: 2, y: 2, z: 4, core: 2. Of those that a mesh axis runs over, the one named last changes fastest.
Arguments:
- anc_inverse: bfloat16 [4, 2, 4, 192, 768], P('pole', None, None, 'col', 'row'), may hold values from -6 to 6
- panel: bfloat16 [4, 2, 768, 1024], P('pole', None, ('row', 'col')), may hold values from -0.21875 to 0.21875
- pattern: int32 [8, 2], replicated, may hold values 0 or 1
- diag_inverse: bfloat16 [4, 2, 1024, 512], P('pole', None, 'col', 'row'), may hold values from -6 to 6
- pole_weights: float32 [4, 2], P('pole'), may hold values from -4 to 4
Outputs:
- inv_panel: float32 [4, 2, 768, 1024], P('pole', None, 'row', 'col')
- inv_diag: bfloat16 [4, 2, 1024, 512], P('pole', None, 'col', 'row')
- density: float32 [1024, 512], P('col', 'row')
All inputs are finite; a program needn't handle non-finite values.
Results may differ from a plain program's by a relative error of at most 0.013.
Values may be sent and summed in bfloat16 or wider, within the bound.
A program may use at most 128 MiB of HBM per device.

v0:
```python
import jax
import jax.numpy as jnp
from jax import lax
from jax.sharding import PartitionSpec as P


def complex_left(left_re, left_im, right_re, right_im):
    upper = jnp.concatenate([left_re, left_im], axis=1)
    lower = jnp.concatenate([-left_im, left_re], axis=1)
    left_side = jnp.concatenate([upper, lower], axis=0)
    right_side = jnp.concatenate([right_re, right_im], axis=0)
    product = lax.dot_general(
        left_side, right_side, (((0,), (0,)), ((), ())), preferred_element_type=jnp.float32
    )
    return product.reshape(2, left_re.shape[1], right_re.shape[1])


def body(anc_inverse, panel, pattern, diag_inverse, pole_weights):
    n_row = lax.axis_size("row")
    n_col = lax.axis_size("col")
    fine_block = lax.axis_index("row") * n_col + lax.axis_index("col")
    pattern_row = lax.dynamic_slice_in_dim(pattern, fine_block, 1, 0)
    block_rows = panel.shape[2]
    width_all = panel.shape[3]
    groups = pattern.shape[1]
    keep_mask = pattern_row.astype(jnp.bfloat16).reshape(1, 1, 1, groups, 1)
    masked = (panel.reshape(1, 2, block_rows, groups, width_all // groups) * keep_mask).reshape(
        1, 2, block_rows, width_all
    )
    local_rows = lax.all_to_all(masked, "col", split_axis=3, concat_axis=2, tiled=True)
    row_count = anc_inverse.shape[4]
    col_count = local_rows.shape[3]
    full_cols = lax.all_gather(local_rows, "row", axis=2, tiled=True)
    stacked = full_cols[0].reshape(2, n_row, block_rows * n_col, col_count)
    segment = lax.all_gather(anc_inverse, "col", axis=3, tiled=True)
    length = segment.shape[3]
    left_side = segment[0].reshape(2, n_row * length, row_count)
    right_side = stacked.reshape(2, n_row * length, col_count)
    summed = complex_left(left_side[0], left_side[1], right_side[0], right_side[1])
    result_panel = -summed
    rounded = result_panel.astype(jnp.bfloat16)
    diag_terms = complex_left(local_rows[0, 0], local_rows[0, 1], rounded[0], rounded[1])
    row_share = lax.psum_scatter(diag_terms, "row", scatter_dimension=2, tiled=True)
    inverse_diag = diag_inverse[0].astype(jnp.float32) - row_share
    pole_weight = pole_weights[0]
    density_term = pole_weight[0] * inverse_diag[1] + pole_weight[1] * inverse_diag[0]
    density = lax.psum(density_term.astype(jnp.bfloat16), "pole").astype(jnp.float32)
    return (result_panel[None], inverse_diag.astype(jnp.bfloat16)[None], density)


def solution(mesh):
    placed = (
        P("pole", None, None, "col", "row"),
        P("pole", None, ("row", "col"), None),
        P(),
        P("pole", None, "col", "row"),
        P("pole", None),
    )
    return jax.shard_map(
        body,
        mesh=mesh,
        in_specs=placed,
        out_specs=(P("pole", None, "row", "col"), P("pole", None, "col", "row"), P("col", "row")),
        check_vma=False,
    )
```

profile of v0, /device:TPU:0, one launch (start us, length us, event | category | flops | bytes accessed | tf_op | source)
XLA Modules:
  0.0 151.4 jit_solution(4732061525736366362)
XLA Ops:
  7.2 0.0 all-gather.2.cloned.1.call-start
  7.2 0.9 fusion.26
  8.1 0.1 broadcast_bitcast_fusion
  8.2 1.0 broadcast_multiply_fusion
  9.2 0.4 copy.12
  9.6 0.0 copy-start.1
  9.6 12.2 %all_to_all.18 = bf16[1,2,96,1024]{2,1,0,3:T(2,128)(2,1)S(1)} all-to-all(bf16[1,2,96,1024]{2,1,0,3:T(2,128)(2,1)S(1)} %copy.12), channel_id=1, replica_groups=mesh['pole'=4,'row'=4,'col'=2] {'col'}, dimensions={3} | all-to-all | bytes 786432 | tf_op jit(solution)/shard_map/all_to_all | solution.py:30
  21.8 0.8 copy.15
  22.6 0.8 copy.14
  23.4 0.0 all-gather.2.cloned.1.call-update
  23.4 0.0 copy-start
  23.4 0.0 reduce-scatter.2.cloned.1.call-start
  23.5 0.0 copy-done.1
  23.5 10.5 %all_gather.6 = bf16[1,2,4,192,192]{4,3,2,1,0:T(8,128)(2,1)S(1)} all-gather(bf16[1,2,4,96,192]{4,3,2,1,0:T(8,128)(2,1)S(1)} %copy-done.1), channel_id=1, replica_groups=mesh['pole'=4,'row'=4,'col'=2] {'col'}, dimensions={3}, use_global_device_ids=true | all-gather | bytes 884736 | tf_op jit(solution)/shard_map/all_gather | solution.py:35
  34.0 0.1 fusion.30
  34.1 0.1 bitcast_negate_fusion
  34.2 26.8 %all-gather.2.cloned.1.call-done = bf16[1,2,768,512]{3,2,1,0:T(8,128)(2,1)} async-done(((bf16[1,2,192,512]{3,2,1,0:T(8,128)(2,1)}), bf16[1,2,768,512]{3,2,1,0:T(8,128)(2,1)}) %all-gather.2.cloned.1.call-update) | async-done | bytes 1572880 | tf_op jit(solution)/shard_map/all_gather | solution.py:33
  61.0 1.5 slice_bitcast_fusion.1
  62.5 1.1 fusion.4
  63.6 0.0 copy-start.4
  63.6 2.1 %fusion.14 = f32[1024,512]{1,0:T(8,128)} fusion(bf16[192,512]{1,0:T(8,128)(2,1)S(1)} %get-tuple-element.10, bf16[192,512]{1,0:T(8,128)(2,1)S(1)} %fusion.29, bf16[192,512]{1,0:T(8,128)(2,1)S(1)} %get-tuple-element.9, f32[384,512]{1,0:T(8,128)S(1)} %fusion.4), kind=kOutput, calls=%fused_computation.14 | convolution fusion | flops 405995520 | bytes 3473408 | tf_op jit(solution)/shard_map/dot_general | solution.py:12
  65.7 0.0 copy-done.4
  65.7 0.0 reduce-scatter.2.cloned.1.call-update
  65.7 0.0 all-reduce.2.cloned.1.call-start
  65.8 0.6 copy-done.3
  66.3 0.6 fusion.31
  67.0 41.4 %reduce-scatter.2.cloned.1.call-done = f32[2,512,128]{2,1,0:T(8,128)} async-done(((f32[2,512,512]{2,1,0:T(8,128)}), f32[2,512,128]{2,1,0:T(8,128)}) %reduce-scatter.2.cloned.1.call-update) | async-done | bytes 524304 | tf_op jit(solution)/shard_map/reduce_scatter | solution.py:43
  108.4 1.8 %convert_bitcast_fusion = (bf16[1,2,512,128]{3,2,1,0:T(8,128)(2,1)}, f32[2,512,128]{2,1,0:T(8,128)S(1)}) fusion(f32[2,512,128]{2,1,0:T(8,128)} %reduce-scatter.2.cloned.1.call-done, bf16[1,2,512,128]{3,2,1,0:T(8,128)(2,1)S(1)} %copy-done.2), kind=kLoop, calls=%fused_computation.28 | loop fusion | flops 393216 | bytes 1572864 | tf_op jit(solution)/shard_map/broadcast_in_dim | solution.py:48
  110.2 1.9 %fusion.25 = bf16[512,128]{1,0:T(8,128)(2,1)} fusion(f32[2,512,128]{2,1,0:T(8,128)S(1)} %get-tuple-element.4, f32[]{:T(128)} %bitcast.14, f32[]{:T(128)} %bitcast.13), kind=kLoop, calls=%fused_computation.32 | loop fusion | flops 262144 | bytes 655368 | tf_op jit(solution)/shard_map/convert_element_type | solution.py:47
  112.1 0.0 all-reduce.2.cloned.1.call-update
  112.1 31.1 %all-reduce.2.cloned.1.call-done = bf16[512,128]{1,0:T(8,128)(2,1)} async-done(((bf16[512,128]{1,0:T(8,128)(2,1)}), bf16[512,128]{1,0:T(8,128)(2,1)}) %all-reduce.2.cloned.1.call-update) | async-done | bytes 131088 | tf_op jit(solution)/shard_map/psum | solution.py:47
  143.2 1.6 %convert_element_type.32 = f32[512,128]{1,0:T(8,128)} convert(bf16[512,128]{1,0:T(8,128)(2,1)} %all-reduce.2.cloned.1.call-done) | non-fusion elementwise | flops 65536 | bytes 393216 | tf_op jit(solution)/shard_map/convert_element_type | solution.py:47
  (7 shorter events, 0.1 us)
Async XLA Ops:
  7.2 53.8 %all-gather.2.cloned.1.call-start = ((), (), s32[]{:S(2)}) async-start(), calls=%async_computation.2 | async-start | bytes 1966080 | tf_op jit(solution)/shard_map/all_gather | solution.py:33
  9.6 13.9 %copy-start.1 = (bf16[1,2,4,96,192]{4,3,2,1,0:T(8,128)(2,1)S(1)}, bf16[1,2,4,96,192]{4,3,2,1,0:T(8,128)(2,1)}, u32[]{:S(2)}) copy-start(bf16[1,2,4,96,192]{4,3,2,1,0:T(8,128)(2,1)} %param.5) | copy-start | bytes 884740
  23.4 10.7 %copy-start = (bf16[1,2,2,96,512]{4,3,2,1,0:T(8,128)(2,1)S(1)}, bf16[1,2,2,96,512]{4,3,2,1,0:T(8,128)(2,1)}, u32[]{:S(2)}) copy-start(bf16[1,2,2,96,512]{4,3,2,1,0:T(8,128)(2,1)} %copy.14) | copy-start | bytes 1179652
  23.4 84.9 %reduce-scatter.2.cloned.1.call-start = ((), (), s32[]{:S(2)}) async-start(), calls=%async_computation.3 | async-start | bytes 2621440 | tf_op jit(solution)/shard_map/reduce_scatter | solution.py:43
  63.6 2.1 %copy-start.4 = (f32[384,512]{1,0:T(8,128)}, f32[384,512]{1,0:T(8,128)S(1)}, u32[]{:S(2)}) copy-start(f32[384,512]{1,0:T(8,128)S(1)} %fusion.4) | copy-start | bytes 2359300
  65.7 0.7 copy-start.3
  65.7 42.7 %copy-start.2 = (bf16[1,2,512,128]{3,2,1,0:T(8,128)(2,1)S(1)}, bf16[1,2,512,128]{3,2,1,0:T(8,128)(2,1)}, u32[]{:S(2)}) copy-start(bf16[1,2,512,128]{3,2,1,0:T(8,128)(2,1)} %param.8) | copy-start | bytes 786436
  65.7 77.5 %all-reduce.2.cloned.1.call-start = ((), (), s32[]{:S(2)}) async-start(), calls=%async_computation.4 | async-start | bytes 262144 | tf_op jit(solution)/shard_map/psum | solution.py:47
Sparse Core Ops, SparseCore 0:
  23.5 37.4 all-gather.1
  65.8 42.5 reduce-scatter.1
  112.2 30.9 all-reduce.1
where the time goes:
time: 152 us; the launch traced here: 151 us
  waiting for transfers between devices  99.4 us (65%)
  blocking collectives  22.7 us (15%)
  between operations  13.8 us (9%)
  other arithmetic  7.29 us (5%)
  local copies, waits for them, and re-layouts  4.86 us (3%)
  matrix products  3.19 us (2%)
    reduce_scatter x1, waiting for transfers between devices, body(): lax.psum_scatter(diag_terms, 'row', scatter_dimension=2, tiled=True)  41.4 us
    psum x1, waiting for transfers between devices, body(): lax.psum(density_term.astype(jnp.bfloat16), 'pole').astype(jnp.float32)  31.1 us
    all_gather x1, waiting for transfers between devices, body(): full_cols = lax.all_gather(local_rows, 'row', axis=2, tiled=True)  26.8 us
    all_to_all x1, blocking collectives, body(): lax.all_to_all(masked, 'col', split_axis=3, concat_axis=2, tiled=True)  12.2 us
    all_gather x1, blocking collectives, body(): segment = lax.all_gather(anc_inverse, 'col', axis=3, tiled=True)  10.5 us
    dot_general x2, matrix products, complex_left(): lax.dot_general(left_side, right_side, (((0,), (0,)), ((), ())), preferre...  3.19 us
  transfers between devices with their start and end apart: 3, of which 3 were waited for; matrix products, arithmetic and copies ran while one was open for 1% of the time, Pallas kernels for 0%

commit v1 on v0

--- a/solution.py
+++ b/solution.py
@@ -30,7 +30,14 @@
     local_rows = lax.all_to_all(masked, "col", split_axis=3, concat_axis=2, tiled=True)
     row_count = anc_inverse.shape[4]
     col_count = local_rows.shape[3]
-    full_cols = lax.all_gather(local_rows, "row", axis=2, tiled=True)
+    count = lax.axis_size("row")
+    right = [(i, (i + 1) % count) for i in range(count)]
+    pieces = [local_rows]
+    for reach in range(1, count):
+        pieces = [lax.ppermute(pieces[0], "row", right), *pieces]
+    out = jnp.concatenate(pieces, axis=2)
+    shift = (lax.axis_index("row") + 1) * pieces[-1].shape[2]
+    full_cols = jnp.roll(out, shift, axis=2)
     stacked = full_cols[0].reshape(2, n_row, block_rows * n_col, col_count)
     segment = lax.all_gather(anc_inverse, "col", axis=3, tiled=True)
     length = segment.shape[3]

time: 152 us -> 144 us (0.947)
  waiting for transfers between devices: 99.4 us -> 91 us
  starting transfers between devices: 0.12 us -> 3.39 us
  local copies, waits for them, and re-layouts: 4.86 us -> 2.66 us
    all_gather x1 -> x0, waiting for transfers between devices: 26.8 us -> none  [body(): full_cols = lax.all_gather(local_rows, 'row', axis=2, tiled=True)]
    ppermute x0 -> x3, waiting for transfers between devices: none -> 19.1 us  [body(): pieces = [lax.ppermute(pieces[0], 'row', right), *pieces]]
    ppermute x0 -> x3, starting transfers between devices: none -> 3.31 us  [body(): pieces = [lax.ppermute(pieces[0], 'row', right), *pieces]]
  transfers between devices with their start and end apart: 3 -> 5, of which waited for: 3 -> 4; matrix products, arithmetic and copies ran while one was open for 1% -> 1% of each run, Pallas kernels for 0% -> 0%
where the time goes in v1:
time: 144 us
  waiting for transfers between devices  91 us (63%)
  blocking collectives  22.2 us (15%)
  between operations  14.2 us (10%)
  other arithmetic  7.39 us (5%)
  starting transfers between devices  3.39 us (2%)
  matrix products  3.18 us (2%)
  local copies, waits for them, and re-layouts  2.66 us (2%)
    reduce_scatter x1, waiting for transfers between devices, body(): lax.psum_scatter(diag_terms, 'row', scatter_dimension=2, tiled=True)  40.8 us
    psum x1, waiting for transfers between devices, body(): lax.psum(density_term.astype(jnp.bfloat16), 'pole').astype(jnp.float32)  31.1 us
    ppermute x3, waiting for transfers between devices, body(): pieces = [lax.ppermute(pieces[0], 'row', right), *pieces]  19.1 us
    all_to_all x1, blocking collectives, body(): lax.all_to_all(masked, 'col', split_axis=3, concat_axis=2, tiled=True)  12 us
    all_gather x1, blocking collectives, body(): segment = lax.all_gather(anc_inverse, 'col', axis=3, tiled=True)  10.2 us
    ppermute x3, starting transfers between devices, body(): pieces = [lax.ppermute(pieces[0], 'row', right), *pieces]  3.31 us
    dot_general x2, matrix products, complex_left(): lax.dot_general(left_side, right_side, (((0,), (0,)), ((), ())), preferre...  3.18 us
  transfers between devices with their start and end apart: 5, of which 4 were waited for; matrix products, arithmetic and copies ran while one was open for 1% of the time, Pallas kernels for 0%

profile of v1, /device:TPU:0, one launch (start us, length us, event | category | flops | bytes accessed | tf_op | source)
XLA Modules:
  0.0 144.1 jit_solution(5131952720708407761)
XLA Ops:
  7.2 0.0 copy-start
  7.2 0.0 reduce-scatter.2.cloned.1.call-start
  7.2 0.9 fusion.26
  8.1 0.1 broadcast_bitcast_fusion
  8.2 1.0 broadcast_multiply_fusion
  9.2 0.4 copy.12
  9.7 12.0 %all_to_all.18 = bf16[1,2,96,1024]{2,1,0,3:T(2,128)(2,1)S(1)} all-to-all(bf16[1,2,96,1024]{2,1,0,3:T(2,128)(2,1)S(1)} %copy.12), channel_id=1, replica_groups=mesh['pole'=4,'row'=4,'col'=2] {'col'}, dimensions={3} | all-to-all | bytes 786432 | tf_op jit(solution)/shard_map/all_to_all | solution.py:30
  21.7 0.8 copy.15
  22.6 1.7 %collective-permute-start = (bf16[1,2,192,512]{3,2,1,0:T(8,128)(2,1)S(1)}, bf16[1,2,192,512]{3,2,1,0:T(8,128)(2,1)S(1)}, u32[]{:S(2)}, u32[]{:S(2)}) collective-permute-start(bf16[1,2,192,512]{3,2,1,0:T(8,128)(2,1)S(1)} %bitcast.31), channel_id=1, source_target_pairs={{0,2},{2,4},{4,6},{6,0},{1,3},{3,5},{5,7},{7,1},{8,10},{10,12},{12... | collective-permute-start | bytes 1179656 | tf_op jit(solution)/shard_map/ppermute | solution.py:37
  24.3 10.2 %all_gather.3 = bf16[1,2,4,192,192]{4,3,2,1,0:T(8,128)(2,1)S(1)} all-gather(bf16[1,2,4,96,192]{4,3,2,1,0:T(8,128)(2,1)S(1)} %copy-done), channel_id=1, replica_groups=mesh['pole'=4,'row'=4,'col'=2] {'col'}, dimensions={3}, use_global_device_ids=true | all-gather | bytes 884736 | tf_op jit(solution)/shard_map/all_gather | solution.py:42
  34.5 0.0 collective-permute-done
  34.5 1.6 %collective-permute-start.1 = (bf16[1,2,192,512]{3,2,1,0:T(8,128)(2,1)S(1)}, bf16[1,2,192,512]{3,2,1,0:T(8,128)(2,1)S(1)}, u32[]{:S(2)}, u32[]{:S(2)}) collective-permute-start(bf16[1,2,192,512]{3,2,1,0:T(8,128)(2,1)S(1)} %collective-permute-done), channel_id=1, source_target_pairs={{0,2},{2,4},{4,6},{6,0},{1,3},{3,5},{5,7},{7,1},{8,10},{10,12},{12... | collective-permute-start | bytes 1179656 | tf_op jit(solution)/shard_map/ppermute | solution.py:37
  36.1 0.1 fusion.30
  36.1 0.1 bitcast_negate_fusion
  36.2 9.1 %collective-permute-done.1 = bf16[1,2,192,512]{3,2,1,0:T(8,128)(2,1)S(1)} collective-permute-done((bf16[1,2,192,512]{3,2,1,0:T(8,128)(2,1)S(1)}, bf16[1,2,192,512]{3,2,1,0:T(8,128)(2,1)S(1)}, u32[]{:S(2)}, u32[]{:S(2)}) %collective-permute-start.1) | collective-permute-done | bytes 393248 | tf_op jit(solution)/shard_map/ppermute | solution.py:37
  45.3 0.0 collective-permute-start.2
  45.4 9.9 %collective-permute-done.2 = bf16[1,2,192,512]{3,2,1,0:T(8,128)(2,1)S(1)} collective-permute-done((bf16[1,2,192,512]{3,2,1,0:T(8,128)(2,1)S(1)}, bf16[1,2,192,512]{3,2,1,0:T(8,128)(2,1)S(1)}, u32[]{:S(2)}, u32[]{:S(2)}) %collective-permute-start.2) | collective-permute-done | bytes 393248 | tf_op jit(solution)/shard_map/ppermute | solution.py:37
  55.6 0.4 dynamic-slice_bitcast_fusion.1
  56.0 1.1 fusion.4
  57.1 0.0 copy-start.3
  57.1 0.0 copy-start.2
  57.1 0.0 copy-start.1
  57.1 2.1 %fusion.14 = f32[1024,512]{1,0:T(8,128)} fusion(bf16[192,512]{1,0:T(8,128)(2,1)S(1)} %get-tuple-element.10, bf16[192,512]{1,0:T(8,128)(2,1)S(1)} %fusion.29, bf16[192,512]{1,0:T(8,128)(2,1)S(1)} %get-tuple-element.9, f32[384,512]{1,0:T(8,128)S(1)} %fusion.4), kind=kOutput, calls=%fused_computation.14 | convolution fusion | flops 405995520 | bytes 3473408 | tf_op jit(solution)/shard_map/dot_general | solution.py:12
  59.2 0.0 reduce-scatter.2.cloned.1.call-update
  59.2 0.0 all-reduce.2.cloned.1.call-start
  59.3 0.6 fusion.31
  59.9 40.8 %reduce-scatter.2.cloned.1.call-done = f32[2,512,128]{2,1,0:T(8,128)} async-done(((f32[2,512,512]{2,1,0:T(8,128)}), f32[2,512,128]{2,1,0:T(8,128)}) %reduce-scatter.2.cloned.1.call-update) | async-done | bytes 524304 | tf_op jit(solution)/shard_map/reduce_scatter | solution.py:50
  100.7 1.8 %convert_bitcast_fusion = (bf16[1,2,512,128]{3,2,1,0:T(8,128)(2,1)}, f32[2,512,128]{2,1,0:T(8,128)S(1)}) fusion(f32[2,512,128]{2,1,0:T(8,128)} %reduce-scatter.2.cloned.1.call-done, bf16[1,2,512,128]{3,2,1,0:T(8,128)(2,1)S(1)} %copy-done.1), kind=kLoop, calls=%fused_computation.28 | loop fusion | flops 393216 | bytes 1572864 | tf_op jit(solution)/shard_map/broadcast_in_dim | solution.py:55
  102.5 2.0 %fusion.25 = bf16[512,128]{1,0:T(8,128)(2,1)} fusion(f32[2,512,128]{2,1,0:T(8,128)S(1)} %get-tuple-element.4, f32[]{:T(128)} %bitcast.14, f32[]{:T(128)} %bitcast.13), kind=kLoop, calls=%fused_computation.32 | loop fusion | flops 262144 | bytes 655368 | tf_op jit(solution)/shard_map/convert_element_type | solution.py:54
  104.5 0.0 all-reduce.2.cloned.1.call-update
  104.5 31.1 %all-reduce.2.cloned.1.call-done = bf16[512,128]{1,0:T(8,128)(2,1)} async-done(((bf16[512,128]{1,0:T(8,128)(2,1)}), bf16[512,128]{1,0:T(8,128)(2,1)}) %all-reduce.2.cloned.1.call-update) | async-done | bytes 131088 | tf_op jit(solution)/shard_map/psum | solution.py:54
  135.6 1.6 %convert_element_type.32 = f32[512,128]{1,0:T(8,128)} convert(bf16[512,128]{1,0:T(8,128)(2,1)} %all-reduce.2.cloned.1.call-done) | non-fusion elementwise | flops 65536 | bytes 393216 | tf_op jit(solution)/shard_map/convert_element_type | solution.py:54
  (16 shorter events, 0.3 us)
Async XLA Ops:
  7.2 17.1 %copy-start = (bf16[1,2,4,96,192]{4,3,2,1,0:T(8,128)(2,1)S(1)}, bf16[1,2,4,96,192]{4,3,2,1,0:T(8,128)(2,1)}, u32[]{:S(2)}) copy-start(bf16[1,2,4,96,192]{4,3,2,1,0:T(8,128)(2,1)} %param.5) | copy-start | bytes 884740
  7.2 93.5 %reduce-scatter.2.cloned.1.call-start = ((), (), s32[]{:S(2)}) async-start(), calls=%async_computation.2 | async-start | bytes 2621440 | tf_op jit(solution)/shard_map/reduce_scatter | solution.py:50
  22.6 11.9 %collective-permute-start = (bf16[1,2,192,512]{3,2,1,0:T(8,128)(2,1)S(1)}, bf16[1,2,192,512]{3,2,1,0:T(8,128)(2,1)S(1)}, u32[]{:S(2)}, u32[]{:S(2)}) collective-permute-start(bf16[1,2,192,512]{3,2,1,0:T(8,128)(2,1)S(1)} %bitcast.31), channel_id=1, source_target_pairs={{0,2},{2,4},{4,6},{6,0},{1,3},{3,5},{5,7},{7,1},{8,10},{10,12},{12... | collective-permute-start | bytes 1179656 | tf_op jit(solution)/shard_map/ppermute | solution.py:37
  34.5 10.8 %collective-permute-start.1 = (bf16[1,2,192,512]{3,2,1,0:T(8,128)(2,1)S(1)}, bf16[1,2,192,512]{3,2,1,0:T(8,128)(2,1)S(1)}, u32[]{:S(2)}, u32[]{:S(2)}) collective-permute-start(bf16[1,2,192,512]{3,2,1,0:T(8,128)(2,1)S(1)} %collective-permute-done), channel_id=1, source_target_pairs={{0,2},{2,4},{4,6},{6,0},{1,3},{3,5},{5,7},{7,1},{8,10},{10,12},{12... | collective-permute-start | bytes 1179656 | tf_op jit(solution)/shard_map/ppermute | solution.py:37
  45.3 10.0 %collective-permute-start.2 = (bf16[1,2,192,512]{3,2,1,0:T(8,128)(2,1)S(1)}, bf16[1,2,192,512]{3,2,1,0:T(8,128)(2,1)S(1)}, u32[]{:S(2)}, u32[]{:S(2)}) collective-permute-start(bf16[1,2,192,512]{3,2,1,0:T(8,128)(2,1)S(1)} %collective-permute-done.1), channel_id=1, source_target_pairs={{0,2},{2,4},{4,6},{6,0},{1,3},{3,5},{5,7},{7,1},{8,10},{10,12},{12... | collective-permute-start | bytes 1179656 | tf_op jit(solution)/shard_map/ppermute | solution.py:37
  57.1 45.4 %copy-start.3 = (f32[384,512]{1,0:T(8,128)}, f32[384,512]{1,0:T(8,128)S(1)}, u32[]{:S(2)}) copy-start(f32[384,512]{1,0:T(8,128)S(1)} %fusion.4) | copy-start | bytes 2359300
  57.1 2.2 %copy-start.2 = (f32[1,2]{1,0:T(1,128)S(1)}, f32[1,2]{1,0:T(1,128)}, u32[]{:S(2)}) copy-start(f32[1,2]{1,0:T(1,128)} %param.9) | copy-start | bytes 28
  57.1 43.6 %copy-start.1 = (bf16[1,2,512,128]{3,2,1,0:T(8,128)(2,1)S(1)}, bf16[1,2,512,128]{3,2,1,0:T(8,128)(2,1)}, u32[]{:S(2)}) copy-start(bf16[1,2,512,128]{3,2,1,0:T(8,128)(2,1)} %param.8) | copy-start | bytes 786436
  59.2 76.4 %all-reduce.2.cloned.1.call-start = ((), (), s32[]{:S(2)}) async-start(), calls=%async_computation.3 | async-start | bytes 262144 | tf_op jit(solution)/shard_map/psum | solution.py:54
Sparse Core Ops, SparseCore 0:
  59.4 41.2 reduce-scatter.1
  104.6 30.9 all-reduce.1
